TPU v7x, 32 devices: a whole 2x2x4 slice. The times are simulated.
32 devices in a mesh: gx: 8 (over z, x), gy: 4 (over y, core).
Axes of the slice: x: 2, y: 2, z: 4, core: 2. Of those that a mesh axis runs over, the one named last changes fastest.
Arguments:
- mode_fields: float32 [32, 512, 1024], P(None, 'gx', 'gy'), may hold values from -60 to 60, as said below
- conductance: float32 [512, 1024], P('gx', 'gy'), may hold values from 0.5 to 2
- potential: float32 [512, 1024], P('gx', 'gy'), may hold values from 0.25 to 4
Outputs:
- basis_field: float32 [128, 512, 1024], P(None, 'gx', 'gy')
- scaled_factor: float32 [128, 128], replicated
Inputs may be any that keep to these rules, and one draw needn't show every extreme that they name: `mode_fields`: Real-valued mode amplitudes.
All inputs are finite; a program needn't handle non-finite values.
Results may differ from a plain program's by a relative error of at most 0.0003.
Values sent between devices are 32-bit elements; how exact they have to be, the bound alone decides.
A program may use at most 64 MiB of HBM per device.

v0:
```python
import jax
import jax.numpy as jnp
from jax import lax
from jax.sharding import PartitionSpec as P


def padded_2(value, sides, width):
    for axis, dim in sides:
        peers, length = (lax.axis_size(axis), value.shape[dim])
        up = [(i, (i + 1) % peers) for i in range(peers - 1)]
        down = [(j, i) for i, j in up]
        last = lax.slice_in_dim(value, length - width, length, axis=dim)
        first = lax.slice_in_dim(value, 0, width, axis=dim)
        before = lax.ppermute(last, axis, up)
        after = lax.ppermute(first, axis, down)
        value = jnp.concatenate([before, value, after], axis=dim)
    return value


def build_columns(fields, conduct, potential):
    center = fields[:, 1:-1, 1:-1]
    k_mid = conduct[1:-1, 1:-1]
    x_plus = 0.5 * (k_mid + conduct[2:, 1:-1])
    x_minus = 0.5 * (k_mid + conduct[:-2, 1:-1])
    y_plus = 0.5 * (k_mid + conduct[1:-1, 2:])
    y_minus = 0.5 * (k_mid + conduct[1:-1, :-2])
    along_x = x_plus * (center - fields[:, 2:, 1:-1]) + x_minus * (center - fields[:, :-2, 1:-1])
    along_y = y_plus * (center - fields[:, 1:-1, 2:]) + y_minus * (center - fields[:, 1:-1, :-2])
    react = potential * center
    stacked = jnp.concatenate([center, along_x, along_y, react], 0)
    return stacked.reshape(stacked.shape[0], -1)


def inner_products(matrix, cell_count):
    return jnp.dot(matrix, matrix.T, precision=lax.Precision.HIGHEST) / cell_count


def on_device(mode_fields, conductance, potential):
    modes_count = mode_fields.shape[0]
    rows_here = mode_fields.shape[1]
    cols_here = mode_fields.shape[2]
    stacked = jnp.concatenate([mode_fields, conductance[None]], 0)
    padded = padded_2(stacked, (("gx", 1), ("gy", 2)), 1)
    matrix = build_columns(padded[:modes_count], padded[modes_count], potential)
    cell_count = float(rows_here * cols_here * lax.axis_size("gx") * lax.axis_size("gy"))
    gram_total = lax.psum(inner_products(matrix, cell_count), ("gx", "gy"))
    lower_tri = jnp.linalg.cholesky(gram_total)
    basis_flat = jax.scipy.linalg.solve_triangular(lower_tri, matrix, lower=True)
    basis_field = basis_flat.reshape(basis_flat.shape[0], rows_here, cols_here)
    return (basis_field, lower_tri.T)


def solution(mesh):
    placed = (P(None, "gx", "gy"), P("gx", "gy"), P("gx", "gy"))
    return jax.shard_map(
        on_device, mesh=mesh, in_specs=placed, out_specs=(P(None, "gx", "gy"), P()), check_vma=False
    )
```

profile of v0, /device:TPU:0, one launch (start us, length us, event | category | flops | bytes accessed | tf_op | source)
XLA Modules:
  0.0 231.3 jit_solution(10538956578714779694)
XLA Ops:
  7.2 0.9 broadcast_in_dim.3
  8.1 5.0 %fusion.22 = (f32[32,64,256]{2,0,1:T(8,128)}, f32[33,64,256]{2,0,1:T(8,128)S(1)}, f32[32,64,256]{2,0,1:T(8,128)}) fusion(f32[32,64,256]{2,1,0:T(8,128)} %param.3, f32[64,256]{1,0:T(8,128)} %param.5), kind=kLoop, calls=%fused_computation.51 | loop fusion | flops 524287 | bytes 8454144 | tf_op args[0]
  13.1 0.9 dynamic-update-slice.4
  14.0 4.9 %collective-permute-start = (f32[33,1,256]{2,0,1:T(8,128)S(1)}, f32[33,1,256]{2,0,1:T(8,128)S(1)}, u32[]{:S(2)}, u32[]{:S(2)}) collective-permute-start(f32[33,1,256]{2,0,1:T(8,128)S(1)} %get-tuple-element.12), channel_id=1, source_target_pairs={{0,4},{4,8},{8,12},{12,16},{16,20},{20,24},{24,28},{1,5},{5,9},{9,... | collective-permute-start | bytes 101384 | tf_op jit(solution)/shard_map/ppermute | solution.py:14
  18.8 1.3 collective-permute-start.1
  20.1 0.4 collective-permute-done
  20.5 4.2 %collective-permute-done.1 = f32[33,1,256]{2,0,1:T(8,128)S(1)} collective-permute-done((f32[33,1,256]{2,0,1:T(8,128)S(1)}, f32[33,1,256]{2,0,1:T(8,128)S(1)}, u32[]{:S(2)}, u32[]{:S(2)}) %collective-permute-start.1) | collective-permute-done | bytes 33824 | tf_op jit(solution)/shard_map/ppermute | solution.py:15
  24.7 0.2 pad_maximum_fusion.1
  24.9 1.9 fusion.20
  26.9 1.8 copy.32
  28.7 1.3 collective-permute-start.3
  30.0 1.8 copy.31
  31.7 3.0 %collective-permute-start.2 = (f32[33,66,1]{1,2,0:T(1,128)S(1)}, f32[33,66,1]{1,2,0:T(1,128)S(1)}, u32[]{:S(2)}, u32[]{:S(2)}) collective-permute-start(f32[33,66,1]{1,2,0:T(1,128)S(1)} %copy.31), channel_id=1, source_target_pairs={{0,1},{1,2},{2,3},{4,5},{5,6},{6,7},{8,9},{9,10},{10,11},{12,13},{... | collective-permute-start | bytes 26144 | tf_op jit(solution)/shard_map/ppermute | solution.py:14
  34.8 1.7 copy.34
  36.5 1.7 copy.33
  38.1 1.5 pad_maximum_fusion.10
  39.8 0.2 copy-done.1
  40.0 0.7 copy-done.2
  40.7 7.0 %fusion.9 = (f32[32,64,256]{2,0,1:T(8,128)}, f32[32,64,256]{2,0,1:T(8,128)}) fusion(f32[33,64,256]{2,0,1:T(8,128)S(1)} %dynamic-update-slice.4, f32[33,1,256]{2,0,1:T(8,128)S(1)} %collective-permute-done, f32[33,1,256]{2,0,1:T(8,128)S(1)} %collective-permute-done.1, f32[64,256]{1,0:T(8,128)S(1)} %get-tuple-element.19, f32[64,256]{1,0:T(8,128)S(1)} %get-tuple-element.17, ...), kind=kLoop, calls=%fused_computation.18 | loop fusion | flops 9437184 | bytes 8801296 | tf_op jit(solution)/shard_map/add | solution.py:27
  47.7 10.7 %fusion.12 = f32[128,128]{0,1:T(8,128)} fusion(f32[32,64,256]{2,0,1:T(8,128)} %get-tuple-element.16, f32[32,64,256]{2,0,1:T(8,128)} %get-tuple-element.9, f32[32,64,256]{2,0,1:T(8,128)} %get-tuple-element.8, f32[32,64,256]{2,0,1:T(8,128)S(1)} %copy-done.3), kind=kOutput, calls=%fused_computation.23 | convolution fusion | flops 3227533312 | bytes 8454144 | tf_op jit(solution)/shard_map/dot_general | solution.py:35
  58.4 5.7 %pad_maximum_fusion = f32[128,64,256]{2,0,1:T(8,128)} fusion(f32[32,64,256]{2,0,1:T(8,128)} %get-tuple-element.16, f32[32,64,256]{2,0,1:T(8,128)} %get-tuple-element.9, f32[32,64,256]{2,0,1:T(8,128)} %get-tuple-element.8, f32[32,64,256]{2,0,1:T(8,128)S(1)} %copy-done.4), kind=kLoop, calls=%fused_computation | loop fusion | flops 6291456 | bytes 16777216 | tf_op jit(solution)/shard_map/concatenate | solution.py:30
  64.1 9.0 %copy.45 = f32[128,64,256]{0,2,1:T(8,128)} copy(f32[128,64,256]{2,0,1:T(8,128)} %pad_maximum_fusion) | data formatting | bytes 16777216 | tf_op jit(solution)/shard_map/concatenate | solution.py:30
  73.1 107.0 %all-reduce.2.cloned.1.call-done = f32[128,128]{0,1:T(8,128)} async-done(((f32[128,128]{0,1:T(8,128)}), f32[128,128]{0,1:T(8,128)}) %all-reduce.2.cloned.1.call-update) | async-done | bytes 65552 | tf_op jit(solution)/shard_map/psum | solution.py:46
  180.1 0.9 copy.44
  181.0 0.9 fusion.18
  181.9 11.7 %cholesky.16 = f32[128,128]{1,0:T(8,128)S(1)} custom-call(f32[128,128]{1,0:T(8,128)S(1)} %fusion.18), custom_call_target="Cholesky" | custom-call | tf_op jit(solution)/shard_map/jit(cholesky)/cholesky | solution.py:47
  193.7 0.6 compare_reduce_fusion
  194.3 0.7 fusion.19
  195.0 0.7 copy.48
  195.7 9.8 %custom-call.7 = f32[1,128,128]{1,2,0:T(8,128)S(1)} custom-call(f32[1,128,128]{2,1,0:T(8,128)S(1)} %get-tuple-element.22), custom_call_target="InvertDiagBlocksLowerTriangular" | custom-call | tf_op jit(solution)/shard_map/jit(_solve_triangular)/triangular_solve | solution.py:48
  205.5 10.7 %fusion = f32[128,64,256]{2,0,1:T(8,128)S(1)} fusion(f32[128,64,256]{0,2,1:T(8,128)} %copy.45, f32[1,128,128]{1,2,0:T(8,128)S(1)} %custom-call.7), kind=kOutput, calls=%fused_computation.1 | convolution fusion | flops 3221225472 | bytes 16842752 | tf_op jit(solution)/shard_map/jit(_solve_triangular)/triangular_solve | solution.py:48
  216.2 8.3 %copy.47 = f32[128,64,256]{2,1,0:T(8,128)} copy(f32[128,64,256]{2,0,1:T(8,128)S(1)} %fusion) | data formatting | bytes 16777216
  (16 shorter events, 0.3 us)
Async XLA Ops:
  7.2 173.0 %all-reduce.2.cloned.1.call-start = ((), (), s32[]{:S(2)}) async-start(), calls=%async_computation | async-start | bytes 131072 | tf_op jit(solution)/shard_map/psum | solution.py:46
  14.0 6.5 %collective-permute-start = (f32[33,1,256]{2,0,1:T(8,128)S(1)}, f32[33,1,256]{2,0,1:T(8,128)S(1)}, u32[]{:S(2)}, u32[]{:S(2)}) collective-permute-start(f32[33,1,256]{2,0,1:T(8,128)S(1)} %get-tuple-element.12), channel_id=1, source_target_pairs={{0,4},{4,8},{8,12},{12,16},{16,20},{20,24},{24,28},{1,5},{5,9},{9,... | collective-permute-start | bytes 101384 | tf_op jit(solution)/shard_map/ppermute | solution.py:14
  18.8 5.9 %collective-permute-start.1 = (f32[33,1,256]{2,0,1:T(8,128)S(1)}, f32[33,1,256]{2,0,1:T(8,128)S(1)}, u32[]{:S(2)}, u32[]{:S(2)}) collective-permute-start(f32[33,1,256]{2,0,1:T(8,128)S(1)} %get-tuple-element.13), channel_id=1, source_target_pairs={{4,0},{8,4},{12,8},{16,12},{20,16},{24,20},{28,24},{5,1},{9,5},{13... | collective-permute-start | bytes 101384 | tf_op jit(solution)/shard_map/ppermute | solution.py:15
  28.7 6.1 %collective-permute-start.3 = (f32[33,66,1]{1,2,0:T(1,128)S(1)}, f32[33,66,1]{1,2,0:T(1,128)S(1)}, u32[]{:S(2)}, u32[]{:S(2)}) collective-permute-start(f32[33,66,1]{1,2,0:T(1,128)S(1)} %copy.32), channel_id=1, source_target_pairs={{1,0},{2,1},{3,2},{5,4},{6,5},{7,6},{9,8},{10,9},{11,10},{13,12},{... | collective-permute-start | bytes 26144 | tf_op jit(solution)/shard_map/ppermute | solution.py:15
  31.7 4.7 %collective-permute-start.2 = (f32[33,66,1]{1,2,0:T(1,128)S(1)}, f32[33,66,1]{1,2,0:T(1,128)S(1)}, u32[]{:S(2)}, u32[]{:S(2)}) collective-permute-start(f32[33,66,1]{1,2,0:T(1,128)S(1)} %copy.31), channel_id=1, source_target_pairs={{0,1},{1,2},{2,3},{4,5},{5,6},{6,7},{8,9},{9,10},{10,11},{12,13},{... | collective-permute-start | bytes 26144 | tf_op jit(solution)/shard_map/ppermute | solution.py:14
  38.1 1.7 copy-start
  38.1 1.9 copy-start.1
  38.1 2.6 %copy-start.2 = (f32[32,64,256]{2,1,0:T(8,128)S(1)}, f32[32,64,256]{2,1,0:T(8,128)}, u32[]{:S(2)}) copy-start(f32[32,64,256]{2,1,0:T(8,128)} %param.3) | copy-start | bytes 6291460
  40.7 7.0 %copy-start.3 = (f32[32,64,256]{2,0,1:T(8,128)S(1)}, f32[32,64,256]{2,0,1:T(8,128)}, u32[]{:S(2)}) copy-start(f32[32,64,256]{2,0,1:T(8,128)} %get-tuple-element.14) | copy-start | bytes 6291460
  47.7 10.7 %copy-start.4 = (f32[32,64,256]{2,0,1:T(8,128)S(1)}, f32[32,64,256]{2,0,1:T(8,128)}, u32[]{:S(2)}) copy-start(f32[32,64,256]{2,0,1:T(8,128)} %get-tuple-element.14) | copy-start | bytes 6291460
Sparse Core Ops, SparseCore 0:
  58.5 121.5 all-reduce.1
where the time goes:
time: 233 us; the launch traced here: 231 us
  waiting for transfers between devices  112 us (48%)
  other arithmetic  43.2 us (19%)
  local copies, waits for them, and re-layouts  30.4 us (13%)
  matrix products  21.4 us (9%)
  between operations  14.2 us (6%)
  starting transfers between devices  10.5 us (5%)
    psum x1, waiting for transfers between devices, on_device(): gram_total = lax.psum(inner_products(matrix, cell_count), ('gx', 'gy'))  107 us
    another operation x3, other arithmetic, on_device(): lower_tri = jnp.linalg.cholesky(gram_total)  12.4 us
    another operation x1, matrix products, on_device(): jax.scipy.linalg.solve_triangular(lower_tri, matrix, lower=True)  10.7 us
    dot_general x1, matrix products, inner_products(): jnp.dot(matrix, matrix.T, precision=lax.Precision.HIGHEST) / cell_count  10.7 us
    unnamed x13, local copies, waits for them, and re-layouts  9.88 us
    another operation x1, other arithmetic, on_device(): jax.scipy.linalg.solve_triangular(lower_tri, matrix, lower=True)  9.81 us
    concatenate x1, local copies, waits for them, and re-layouts, build_columns(): stacked = jnp.concatenate([center, along_x, along_y, react], 0)  9 us
    ppermute x2, starting transfers between devices, padded_2(): before = lax.ppermute(last, axis, up)  7.91 us
  transfers between devices with their start and end apart: 5, of which 3 were waited for; matrix products, arithmetic and copies ran while one was open for 8% of the time, Pallas kernels for 0%

commit v1 on v0

v1 whole, which is shorter than its diff:
```python
import functools

import jax
import jax.numpy as jnp
from jax import lax
from jax.experimental import pallas as pl
from jax.experimental.pallas import tpu as pltpu
from jax.sharding import PartitionSpec as P

MESH = pl.DeviceIdType.MESH
F32 = jnp.float32
BF16 = jnp.bfloat16


def split(value):
    high = value.astype(BF16)
    return high, (value - high.astype(F32)).astype(BF16)


def gram_kernel(
    nx, ny, u_hbm, k_ref, p_ref, m_ref, g_ref,
    flat, load, wide, edge, halo, acc, part, piece, ring, full,
    halo_send, halo_recv, rs_send, rs_recv, all_send, all_recv, ag_send, ag_recv,
):
    rows, cols = k_ref.shape
    modes = u_hbm.shape[0] // rows
    tiles = cols // 128
    columns = 4 * modes
    share = columns // ny
    px, py = lax.axis_index("gx"), lax.axis_index("gy")

    loads = [
        pltpu.make_async_copy(u_hbm.at[:, pl.ds(t * 128, 128)], flat.at[t], load.at[t]) for t in range(tiles)
    ]
    for copy in loads:
        copy.start()
    barrier = pltpu.get_barrier_semaphore()
    for d in range(1, nx):
        pl.semaphore_signal(barrier, inc=1, device_id={"gx": lax.rem(px + d, nx)}, device_id_type=MESH)
    for d in range(1, ny):
        pl.semaphore_signal(barrier, inc=1, device_id={"gy": lax.rem(py + d, ny)}, device_id_type=MESH)

    lanes = lax.broadcasted_iota(jnp.int32, (modes + 8, 128), 1)

    def spread(i, carry):
        first, last = carry
        row = jnp.concatenate(
            [jnp.concatenate([flat[t, pl.ds(i, modes, stride=rows), :] for t in range(tiles)], 1),
             jnp.broadcast_to(k_ref[pl.ds(i, 1), :], (8, cols))], 0
        )
        wide[i + 1] = row
        first = jnp.where(lanes == i, pltpu.roll(row[:, :128], i, 1), first)
        last = jnp.where(lanes == i, pltpu.roll(row[:, cols - 128:], lax.rem(i + 1, 128), 1), last)
        return first, last

    for copy in loads:
        copy.wait()
    zero = jnp.zeros((modes + 8, 128), F32)
    first, last = lax.fori_loop(0, rows, spread, (zero, zero), unroll=4)
    edge[0] = first
    edge[1] = last

    pl.semaphore_wait(barrier, nx + ny - 2)
    right, left = lax.rem(py + 1, ny), lax.rem(py + ny - 1, ny)
    down, up = lax.rem(px + 1, nx), lax.rem(px + nx - 1, nx)
    moves = (
        (edge.at[1], halo.at[0], {"gy": right}),
        (edge.at[0], halo.at[1], {"gy": left}),
        (wide.at[rows], wide.at[0], {"gx": down}),
        (wide.at[1], wide.at[rows + 1], {"gx": up}),
    )
    copies = [
        pltpu.make_async_remote_copy(
            src_ref=src, dst_ref=dst, send_sem=halo_send.at[n], recv_sem=halo_recv.at[n],
            device_id=device, device_id_type=MESH,
        )
        for n, (src, dst, device) in enumerate(moves)
    ]
    for copy in copies:
        copy.start()
    for copy in copies:
        copy.wait()
    wide[0] = jnp.where(px > 0, wide[0], 0.0)
    wide[rows + 1] = jnp.where(px < nx - 1, wide[rows + 1], 0.0)
    halo[0] = jnp.where(py > 0, halo[0], 0.0)
    halo[1] = jnp.where(py < ny - 1, halo[1], 0.0)

    group = 4
    span = lax.broadcasted_iota(jnp.int32, (modes + 8, cols), 1)
    acc[...] = jnp.zeros_like(acc)

    def build(g, _):
        for s in range(group):
            i = g * group + s
            row = wide[i + 1]
            center, k_mid = row[:modes], row[modes:modes + 1]
            after, before = wide[i + 2], wide[i]
            pad = jnp.zeros((modes + 8, cols - 128), F32)
            left_edge = jnp.concatenate([pltpu.roll(halo[0], lax.rem(128 - i, 128), 1), pad], 1)
            right_edge = jnp.concatenate([pad, pltpu.roll(halo[1], 127 - i, 1)], 1)
            to_left = jnp.where(span == 0, left_edge, pltpu.roll(row, 1, 1))
            to_right = jnp.where(span == cols - 1, right_edge, pltpu.roll(row, cols - 1, 1))
            along_x = (0.5 * (k_mid + after[modes:modes + 1])) * (center - after[:modes]) + (
                0.5 * (k_mid + before[modes:modes + 1])
            ) * (center - before[:modes])
            along_y = (0.5 * (k_mid + to_right[modes:modes + 1])) * (center - to_right[:modes]) + (
                0.5 * (k_mid + to_left[modes:modes + 1])
            ) * (center - to_left[:modes])
            react = p_ref[pl.ds(i, 1), :] * center
            high, low = split(jnp.concatenate([center, along_x, along_y, react], 0))
            for t in range(tiles):
                at = pl.ds(pl.multiple_of((t * rows + i) * 128, 128), 128)
                m_ref[:columns, at] = high[:, t * 128:(t + 1) * 128]
                m_ref[columns:, at] = low[:, t * 128:(t + 1) * 128]
        for t in range(tiles):
            at = pl.ds(pl.multiple_of((t * rows + g * group) * 128, group * 128), group * 128)
            acc[...] += lax.dot_general(
                m_ref[:columns, at], m_ref[:, at], (((1,), (1,)), ((), ())), preferred_element_type=F32
            )
        return 0

    lax.fori_loop(0, rows // group, build, 0)
    cross = acc[:, columns:]
    total = (acc[:, :columns] + (cross + cross.T)) * (1.0 / (rows * cols * nx * ny))
    for j in range(ny):
        part[j] = total[j * share:(j + 1) * share]

    copies = [
        pltpu.make_async_remote_copy(
            src_ref=part.at[lax.rem(py + d, ny)], dst_ref=piece.at[py], send_sem=rs_send.at[d], recv_sem=rs_recv.at[d],
            device_id={"gy": lax.rem(py + d, ny)}, device_id_type=MESH,
        )
        for d in range(1, ny)
    ]
    for copy in copies:
        copy.start()
    piece[py] = part[py]
    for copy in copies:
        copy.wait()
    ring[px] = functools.reduce(jnp.add, [piece[j] for j in range(ny)])

    copies = [
        pltpu.make_async_remote_copy(
            src_ref=ring.at[px], dst_ref=ring.at[px], send_sem=all_send.at[d], recv_sem=all_recv.at[d],
            device_id={"gx": lax.rem(px + d, nx)}, device_id_type=MESH,
        )
        for d in range(1, nx)
    ]
    for copy in copies:
        copy.start()
    for copy in copies:
        copy.wait()
    full[py] = functools.reduce(jnp.add, [ring[j] for j in range(nx)])

    copies = [
        pltpu.make_async_remote_copy(
            src_ref=full.at[py], dst_ref=full.at[py], send_sem=ag_send.at[d], recv_sem=ag_recv.at[d],
            device_id={"gy": lax.rem(py + d, ny)}, device_id_type=MESH,
        )
        for d in range(1, ny)
    ]
    for copy in copies:
        copy.start()
    for copy in copies:
        copy.wait()
    for j in range(ny):
        g_ref[j * share:(j + 1) * share, :] = full[j]


def gram(fields, conduct, potential, nx, ny):
    modes, rows, cols = fields.shape
    columns = 4 * modes
    vmem = pl.BlockSpec(memory_space=pltpu.VMEM)
    dma = pltpu.SemaphoreType.DMA
    return pl.pallas_call(
        functools.partial(gram_kernel, nx, ny),
        out_shape=(
            jax.ShapeDtypeStruct((2 * columns, rows * cols), BF16),
            jax.ShapeDtypeStruct((columns, columns), F32),
        ),
        in_specs=[pl.BlockSpec(memory_space=pl.ANY), vmem, vmem],
        out_specs=(vmem, vmem),
        scratch_shapes=[
            pltpu.VMEM((cols // 128, modes * rows, 128), F32),
            dma((cols // 128,)),
            pltpu.VMEM((rows + 2, modes + 8, cols), F32),
            pltpu.VMEM((2, modes + 8, 128), F32),
            pltpu.VMEM((2, modes + 8, 128), F32),
            pltpu.VMEM((columns, 2 * columns), F32),
            pltpu.VMEM((ny, columns // ny, columns), F32),
            pltpu.VMEM((ny, columns // ny, columns), F32),
            pltpu.VMEM((nx, columns // ny, columns), F32),
            pltpu.VMEM((ny, columns // ny, columns), F32),
            dma((4,)), dma((4,)), dma((ny,)), dma((ny,)), dma((nx,)), dma((nx,)), dma((ny,)), dma((ny,)),
        ],
        compiler_params=pltpu.CompilerParams(
            collective_id=0, has_side_effects=True, vmem_limit_bytes=28 * 1024 * 1024
        ),
        name="gram",
    )(fields.reshape(modes * rows, cols), conduct, potential)


def apply_kernel(w_ref, m_ref, o_ref):
    columns, chunk, _ = o_ref.shape
    high, low = split(w_ref[...])
    weights = jnp.concatenate(
        [jnp.concatenate([high, high], 1), jnp.concatenate([low, jnp.zeros_like(low)], 1)], 0
    )
    flat = o_ref.reshape(columns * chunk, 128)
    for s in range(0, chunk, 2):
        both = jnp.dot(weights, m_ref[:, s * 128:(s + 2) * 128], preferred_element_type=F32)
        out = both[:columns] + both[columns:]
        for r in range(2):
            flat[pl.ds(s + r, columns, stride=chunk), :] = out[:, r * 128:(r + 1) * 128]


def apply(inverse, matrix, rows, cols):
    columns = inverse.shape[0]
    chunk = 16
    steps = rows // chunk
    return pl.pallas_call(
        apply_kernel,
        out_shape=jax.ShapeDtypeStruct((columns, rows, cols), F32),
        grid=(cols // 128, steps),
        in_specs=[
            pl.BlockSpec((columns, columns), lambda t, i: (0, 0)),
            pl.BlockSpec((2 * columns, chunk * 128), lambda t, i: (0, t * steps + i)),
        ],
        out_specs=pl.BlockSpec((columns, chunk, 128), lambda t, i: (0, i, t)),
        compiler_params=pltpu.CompilerParams(vmem_limit_bytes=16 * 1024 * 1024),
        name="apply",
    )(inverse, matrix)


def on_device(nx, ny, mode_fields, conductance, potential):
    modes, rows, cols = mode_fields.shape
    matrix, total = gram(mode_fields, conductance, potential, nx, ny)
    lower_tri = jnp.linalg.cholesky(total, symmetrize_input=False)
    inverse = jax.scipy.linalg.solve_triangular(lower_tri, jnp.eye(4 * modes, dtype=F32), lower=True)
    return apply(inverse, matrix, rows, cols), lower_tri.T


def solution(mesh):
    placed = (P(None, "gx", "gy"), P("gx", "gy"), P("gx", "gy"))
    return jax.shard_map(
        functools.partial(on_device, mesh.shape["gx"], mesh.shape["gy"]),
        mesh=mesh, in_specs=placed, out_specs=(P(None, "gx", "gy"), P()), check_vma=False,
    )
```

time: 233 us -> 71.9 us (0.31)
  waiting for transfers between devices: 112 us -> 0 us
  Pallas kernels: 0 us -> 37 us
  matrix products: 21.4 us -> 0.25 us
  other arithmetic: 43.2 us -> 22.9 us
  local copies, waits for them, and re-layouts: 30.4 us -> 10.8 us
  between operations: 14.2 us -> 0.68 us
  starting transfers between devices: 10.5 us -> 0 us
    psum x1 -> x0, waiting for transfers between devices: 107 us -> none  [on_device(): gram_total = lax.psum(inner_products(matrix, cell_count), ('gx', 'gy'))]
    pallas_call x0 -> x2, Pallas kernels: none -> 37 us  [the longest x1 30.2 us: gram(): pl.pallas_call(functools.partial(gram_kernel, nx, ny), out_shape=(jax.Sha...]
    dot_general x1 -> x0, matrix products: 10.7 us -> none  [inner_products(): jnp.dot(matrix, matrix.T, precision=lax.Precision.HIGHEST) / cell_count]
    ppermute x4 -> x0, starting transfers between devices: 10.5 us -> none  [the longest x2 7.91 us: padded_2(): before = lax.ppermute(last, axis, up)]
    another operation x1, matrix products: 10.7 us -> 0.25 us  [on_device(): jax.scipy.linalg.solve_triangular(lower_tri, jnp.eye(4 * modes, dtype=F32...]
    concatenate x2 -> x0, local copies, waits for them, and re-layouts: 9.87 us -> none  [the longest x1 9 us: build_columns(): stacked = jnp.concatenate([center, along_x, along_y, react], 0)]
    concatenate x3 -> x0, other arithmetic: 7.4 us -> none  [the longest x1 5.69 us: build_columns(): stacked = jnp.concatenate([center, along_x, along_y, react], 0)]
    add x1 -> x0, other arithmetic: 6.99 us -> none  [build_columns(): x_plus * (center - fields[:, 2:, 1:-1])]
  transfers between devices with their start and end apart: 5 -> 0, of which waited for: 3 -> 0; matrix products, arithmetic and copies ran while one was open for 8% -> 0% of each run, Pallas kernels for 0% -> 0%
where the time goes in v1:
time: 71.9 us; the launch traced here: 71.6 us
  Pallas kernels  37 us (51%)
  other arithmetic  22.9 us (32%)
  local copies, waits for them, and re-layouts  10.8 us (15%)
    pallas_call x1, Pallas kernels, gram(): pl.pallas_call(functools.partial(gram_kernel, nx, ny), out_shape=(jax.Sha...  30.2 us
    another operation x3, other arithmetic, on_device(): lower_tri = jnp.linalg.cholesky(total, symmetrize_input=False)  12.4 us
    unnamed x11, local copies, waits for them, and re-layouts  10.8 us
    another operation x1, other arithmetic, on_device(): jax.scipy.linalg.solve_triangular(lower_tri, jnp.eye(4 * modes, dtype=F32...  9.81 us
    pallas_call x1, Pallas kernels, apply(): pl.pallas_call(apply_kernel, out_shape=jax.ShapeDtypeStruct((columns, row...  6.8 us

profile of v1, /device:TPU:0, one launch (start us, length us, event | category | flops | bytes accessed | tf_op | source)
XLA Modules:
  0.0 71.6 jit_solution(4145420034960511929)
XLA Ops:
  0.6 0.0 copy-start.2
  0.6 1.6 %copy-done.2 = f32[32,64,256]{2,1,0:T(8,128)S(1)} copy-done((f32[32,64,256]{2,1,0:T(8,128)S(1)}, f32[32,64,256]{2,1,0:T(8,128)}, u32[]{:S(2)}) %copy-start.2) | copy-done | bytes 2097176
  2.2 0.0 copy-start.3
  2.2 0.8 %copy-done.3 = f32[64,256]{1,0:T(8,128)S(1)} copy-done((f32[64,256]{1,0:T(8,128)S(1)}, f32[64,256]{1,0:T(8,128)}, u32[]{:S(2)}) %copy-start.3) | copy-done | bytes 65560
  3.1 0.0 copy-start.4
  3.1 0.8 %copy-done.4 = f32[64,256]{1,0:T(8,128)S(1)} copy-done((f32[64,256]{1,0:T(8,128)S(1)}, f32[64,256]{1,0:T(8,128)}, u32[]{:S(2)}) %copy-start.4) | copy-done | bytes 65560
  3.9 30.2 %gram.1 = (bf16[256,16384]{1,0:T(8,128)(2,1)S(1)}, f32[128,128]{1,0:T(8,128)S(1)}) custom-call(f32[2048,256]{1,0:T(8,128)S(1)} %bitcast.8, f32[64,256]{1,0:T(8,128)S(1)} %copy-done.3, f32[64,256]{1,0:T(8,128)S(1)} %copy-done.4), custom_call_target="tpu_custom_call" | custom-call | tf_op jit(solution)/shard_map/gram/pallas_call | solution.py:175
  34.1 0.0 copy-start
  34.2 3.4 %copy-done = bf16[256,16384]{1,0:T(8,128)(2,1)} copy-done((bf16[256,16384]{1,0:T(8,128)(2,1)}, bf16[256,16384]{1,0:T(8,128)(2,1)S(1)}, u32[]{:S(2)}) %copy-start) | copy-done | bytes 8388632
  37.5 11.7 %cholesky.17 = f32[128,128]{1,0:T(8,128)S(1)} custom-call(f32[128,128]{1,0:T(8,128)S(1)} %get-tuple-element.4), custom_call_target="Cholesky" | custom-call | tf_op jit(solution)/shard_map/jit(cholesky)/cholesky | solution.py:238
  49.3 0.6 compare_reduce_fusion
  49.9 0.7 fusion.2
  50.6 0.7 %copy.5 = f32[128,128]{1,0:T(8,128)} copy(f32[128,128]{0,1:T(8,128)S(1)} %get-tuple-element.8) | data formatting | bytes 131072
  51.3 9.8 %custom-call.7 = f32[1,128,128]{1,2,0:T(8,128)S(1)} custom-call(f32[1,128,128]{2,1,0:T(8,128)S(1)} %get-tuple-element.9), custom_call_target="InvertDiagBlocksLowerTriangular" | custom-call | tf_op jit(solution)/shard_map/jit(_solve_triangular)/triangular_solve | solution.py:239
  61.1 0.2 fusion.w_ref
  61.4 0.0 copy-start.1
  61.4 3.4 %copy-done.1 = bf16[256,16384]{1,0:T(8,128)(2,1)S(1)} copy-done((bf16[256,16384]{1,0:T(8,128)(2,1)S(1)}, bf16[256,16384]{1,0:T(8,128)(2,1)}, u32[]{:S(2)}) %copy-start.1) | copy-done | bytes 8388632
  64.8 6.8 %apply.1 = f32[128,64,256]{2,1,0:T(8,128)} custom-call(f32[128,128]{1,0:T(8,128)S(1)} %fusion.w_ref, bf16[256,16384]{1,0:T(8,128)(2,1)S(1)} %copy-done.1), custom_call_target="tpu_custom_call" | custom-call | tf_op jit(solution)/shard_map/apply/pallas_call | solution.py:221
  (1 shorter events, 0.0 us)
Async XLA Ops:
  0.6 1.6 %copy-start.2 = (f32[32,64,256]{2,1,0:T(8,128)S(1)}, f32[32,64,256]{2,1,0:T(8,128)}, u32[]{:S(2)}) copy-start(f32[32,64,256]{2,1,0:T(8,128)} %param.3) | copy-start | bytes 6291460
  2.2 0.8 %copy-start.3 = (f32[64,256]{1,0:T(8,128)S(1)}, f32[64,256]{1,0:T(8,128)}, u32[]{:S(2)}) copy-start(f32[64,256]{1,0:T(8,128)} %k_ref.1) | copy-start | bytes 196612
  3.1 0.8 %copy-start.4 = (f32[64,256]{1,0:T(8,128)S(1)}, f32[64,256]{1,0:T(8,128)}, u32[]{:S(2)}) copy-start(f32[64,256]{1,0:T(8,128)} %p_ref.1) | copy-start | bytes 196612
  34.1 3.4 %copy-start = (bf16[256,16384]{1,0:T(8,128)(2,1)}, bf16[256,16384]{1,0:T(8,128)(2,1)S(1)}, u32[]{:S(2)}) copy-start(bf16[256,16384]{1,0:T(8,128)(2,1)S(1)} %get-tuple-element.5.m_ref) | copy-start | bytes 25165828
  61.4 3.4 %copy-start.1 = (bf16[256,16384]{1,0:T(8,128)(2,1)S(1)}, bf16[256,16384]{1,0:T(8,128)(2,1)}, u32[]{:S(2)}) copy-start(bf16[256,16384]{1,0:T(8,128)(2,1)} %copy-done) | copy-start | bytes 25165828

commit v2 on v1

--- a/solution.py
+++ b/solution.py
@@ -18,11 +18,11 @@
 
 
 def gram_kernel(
-    nx, ny, u_hbm, k_ref, p_ref, m_ref, g_ref,
-    flat, load, wide, edge, halo, acc, part, piece, ring, full,
+    nx, ny, u_hbm, k_hbm, p_hbm, m_ref, g_ref,
+    k_ref, p_ref, flat, load, wide, edge, halo, acc, part, piece, ring, full,
     halo_send, halo_recv, rs_send, rs_recv, all_send, all_recv, ag_send, ag_recv,
 ):
-    rows, cols = k_ref.shape
+    rows, cols = k_hbm.shape
     modes = u_hbm.shape[0] // rows
     tiles = cols // 128
     columns = 4 * modes
@@ -32,6 +32,8 @@
     loads = [
         pltpu.make_async_copy(u_hbm.at[:, pl.ds(t * 128, 128)], flat.at[t], load.at[t]) for t in range(tiles)
     ]
+    loads.append(pltpu.make_async_copy(k_hbm, k_ref, load.at[tiles]))
+    loads.append(pltpu.make_async_copy(p_hbm, p_ref, load.at[tiles + 1]))
     for copy in loads:
         copy.start()
     barrier = pltpu.get_barrier_semaphore()
@@ -178,11 +180,13 @@
             jax.ShapeDtypeStruct((2 * columns, rows * cols), BF16),
             jax.ShapeDtypeStruct((columns, columns), F32),
         ),
-        in_specs=[pl.BlockSpec(memory_space=pl.ANY), vmem, vmem],
+        in_specs=[pl.BlockSpec(memory_space=pltpu.HBM)] * 3,
         out_specs=(vmem, vmem),
         scratch_shapes=[
+            pltpu.VMEM((rows, cols), F32),
+            pltpu.VMEM((rows, cols), F32),
             pltpu.VMEM((cols // 128, modes * rows, 128), F32),
-            dma((cols // 128,)),
+            dma((cols // 128 + 2,)),
             pltpu.VMEM((rows + 2, modes + 8, cols), F32),
             pltpu.VMEM((2, modes + 8, 128), F32),
             pltpu.VMEM((2, modes + 8, 128), F32),
@@ -194,50 +198,109 @@
             dma((4,)), dma((4,)), dma((ny,)), dma((ny,)), dma((nx,)), dma((nx,)), dma((ny,)), dma((ny,)),
         ],
         compiler_params=pltpu.CompilerParams(
-            collective_id=0, has_side_effects=True, vmem_limit_bytes=28 * 1024 * 1024
+            collective_id=0, has_side_effects=True, vmem_limit_bytes=66_900_000 - 4 * columns * rows * cols
         ),
         name="gram",
     )(fields.reshape(modes * rows, cols), conduct, potential)
 
 
-def apply_kernel(w_ref, m_ref, o_ref):
+def factor(g_ref, r_ref, w_ref):
+    size = g_ref.shape[0]
+    block = 8
+    panels = size // block
+    lane = lax.broadcasted_iota(jnp.int32, (block, size), 1)
+    sub = lax.broadcasted_iota(jnp.int32, (block, size), 0)
+
+    def stack(values):
+        out = values[0]
+        for j in range(1, block):
+            out = jnp.where(sub == j, values[j], out)
+        return out
+
+    def row(value, j):
+        return jnp.broadcast_to(value[j:j + 1], (block, size))
+
+    def column(value, j):
+        return jnp.broadcast_to(value[:, j:j + 1], (block, size))
+
+    z = [g_ref[i * block:(i + 1) * block, :] for i in range(panels)]
+    for p in range(panels):
+        at = p * block
+        diag = [column(z[p], at + j) for j in range(block)]
+        a = [[row(diag[j], i) for j in range(i + 1)] for i in range(block)]
+        low = [[None] * block for _ in range(block)]
+        inv = [[None] * block for _ in range(block)]
+        for j in range(block):
+            root = lax.rsqrt(a[j][j])
+            inv[j][j] = root
+            for i in range(j + 1, block):
+                low[i][j] = a[i][j] * root
+            for i in range(j + 1, block):
+                for k in range(j + 1, i + 1):
+                    a[i][k] = a[i][k] - low[i][j] * low[k][j]
+            for k in range(j):
+                terms = [low[j][q] * inv[q][k] for q in range(k, j)]
+                inv[j][k] = -root * functools.reduce(jnp.add, terms)
+        inside = (lane >= at) & (lane < at + block)
+        source = [row(z[p], k) for k in range(block)]
+        swept = [jnp.where(inside, jnp.where(lane == at + k, 1.0, 0.0), source[k]) for k in range(block)]
+        solved = [functools.reduce(jnp.add, [inv[j][k] * swept[k] for k in range(j + 1)]) for j in range(block)]
+        upper = [functools.reduce(jnp.add, [inv[j][k] * source[k] for k in range(j + 1)]) for j in range(block)]
+        r_ref[at:at + block, :] = jnp.where(lane >= at + sub, stack(upper), 0.0)
+        w_ref[at:at + block, :] = jnp.where(lane <= at + sub, stack(solved), 0.0)
+        if p + 1 < panels:
+            both = [
+                functools.reduce(jnp.add, [inv[j][k] * solved[j] for j in range(k, block)]) for k in range(block)
+            ]
+            for i in range(p + 1, panels):
+                terms = [column(z[i], at + k) * both[k] for k in range(block)]
+                z[i] = jnp.where(inside, 0.0, z[i]) - functools.reduce(jnp.add, terms)
+
+
+def apply_kernel(g_ref, m_ref, o_ref, r_ref, w_ref, weights):
     columns, chunk, _ = o_ref.shape
-    high, low = split(w_ref[...])
-    weights = jnp.concatenate(
-        [jnp.concatenate([high, high], 1), jnp.concatenate([low, jnp.zeros_like(low)], 1)], 0
-    )
+
+    @pl.when((pl.program_id(0) == 0) & (pl.program_id(1) == 0))
+    def _():
+        factor(g_ref, r_ref, w_ref)
+        high, low = split(w_ref[...])
+        weights[:columns, :columns] = high
+        weights[:columns, columns:] = high
+        weights[columns:, :columns] = low
+        weights[columns:, columns:] = jnp.zeros_like(low)
+
     flat = o_ref.reshape(columns * chunk, 128)
     for s in range(0, chunk, 2):
-        both = jnp.dot(weights, m_ref[:, s * 128:(s + 2) * 128], preferred_element_type=F32)
+        both = jnp.dot(weights[...], m_ref[:, s * 128:(s + 2) * 128], preferred_element_type=F32)
         out = both[:columns] + both[columns:]
         for r in range(2):
             flat[pl.ds(s + r, columns, stride=chunk), :] = out[:, r * 128:(r + 1) * 128]
 
 
-def apply(inverse, matrix, rows, cols):
-    columns = inverse.shape[0]
+def apply(total, matrix, rows, cols):
+    columns = total.shape[0]
     chunk = 16
     steps = rows // chunk
+    square = pl.BlockSpec((columns, columns), lambda t, i: (0, 0))
     return pl.pallas_call(
         apply_kernel,
-        out_shape=jax.ShapeDtypeStruct((columns, rows, cols), F32),
+        out_shape=(
+            jax.ShapeDtypeStruct((columns, rows, cols), F32),
+            jax.ShapeDtypeStruct((columns, columns), F32),
+        ),
         grid=(cols // 128, steps),
-        in_specs=[
-            pl.BlockSpec((columns, columns), lambda t, i: (0, 0)),
-            pl.BlockSpec((2 * columns, chunk * 128), lambda t, i: (0, t * steps + i)),
-        ],
-        out_specs=pl.BlockSpec((columns, chunk, 128), lambda t, i: (0, i, t)),
+        in_specs=[square, pl.BlockSpec((2 * columns, chunk * 128), lambda t, i: (0, t * steps + i))],
+        out_specs=(pl.BlockSpec((columns, chunk, 128), lambda t, i: (0, i, t)), square),
+        scratch_shapes=[pltpu.VMEM((columns, columns), F32), pltpu.VMEM((2 * columns, 2 * columns), BF16)],
         compiler_params=pltpu.CompilerParams(vmem_limit_bytes=16 * 1024 * 1024),
         name="apply",
-    )(inverse, matrix)
+    )(total, matrix)
 
 
 def on_device(nx, ny, mode_fields, conductance, potential):
-    modes, rows, cols = mode_fields.shape
+    _, rows, cols = mode_fields.shape
     matrix, total = gram(mode_fields, conductance, potential, nx, ny)
-    lower_tri = jnp.linalg.cholesky(total, symmetrize_input=False)
-    inverse = jax.scipy.linalg.solve_triangular(lower_tri, jnp.eye(4 * modes, dtype=F32), lower=True)
-    return apply(inverse, matrix, rows, cols), lower_tri.T
+    return apply(total, matrix, rows, cols)
 
 
 def solution(mesh):

time: 71.9 us -> 51.4 us (0.71)
  other arithmetic: 22.9 us -> 0 us
  Pallas kernels: 37 us -> 46.3 us
  local copies, waits for them, and re-layouts: 10.8 us -> 4.21 us
    another operation x4 -> x0, other arithmetic: 22.2 us -> none  [the longest x3 12.4 us: on_device(): lower_tri = jnp.linalg.cholesky(total, symmetrize_input=False)]
    unnamed x11 -> x4, local copies, waits for them, and re-layouts: 10.8 us -> 4.21 us
    pallas_call x1, Pallas kernels: 6.8 us -> 11.5 us  [apply(): pl.pallas_call(apply_kernel, out_shape=(jax.ShapeDtypeStruct((columns, ro...]
    pallas_call x1, Pallas kernels: 30.2 us -> 34.7 us  [gram(): pl.pallas_call(functools.partial(gram_kernel, nx, ny), out_shape=(jax.Sha...]
where the time goes in v2:
time: 51.4 us; the launch traced here: 51.1 us
  Pallas kernels  46.3 us (90%)
  local copies, waits for them, and re-layouts  4.21 us (8%)
  between operations  0.65 us (1%)
    pallas_call x1, Pallas kernels, gram(): pl.pallas_call(functools.partial(gram_kernel, nx, ny), out_shape=(jax.Sha...  34.7 us
    pallas_call x1, Pallas kernels, apply(): pl.pallas_call(apply_kernel, out_shape=(jax.ShapeDtypeStruct((columns, ro...  11.5 us
    unnamed x4, local copies, waits for them, and re-layouts  4.21 us

profile of v2, /device:TPU:0, one launch (start us, length us, event | category | flops | bytes accessed | tf_op | source)
XLA Modules:
  0.0 51.1 jit_solution(8416664565004951202)
XLA Ops:
  0.6 34.7 %gram.1 = (bf16[256,16384]{1,0:T(8,128)(2,1)}, f32[128,128]{1,0:T(8,128)}) custom-call(f32[2048,256]{1,0:T(8,128)} %bitcast.1, f32[64,256]{1,0:T(8,128)} %k_hbm.1, f32[64,256]{1,0:T(8,128)} %p_hbm.1), custom_call_target="tpu_custom_call" | custom-call | tf_op jit(solution)/shard_map/gram/pallas_call | solution.py:177
  35.4 0.0 copy-start
  35.4 3.4 %copy-done = bf16[256,16384]{1,0:T(8,128)(2,1)S(1)} copy-done((bf16[256,16384]{1,0:T(8,128)(2,1)S(1)}, bf16[256,16384]{1,0:T(8,128)(2,1)}, u32[]{:S(2)}) %copy-start) | copy-done | bytes 8388632
  38.8 0.0 copy-start.1
  38.8 0.8 %copy-done.1 = f32[128,128]{1,0:T(8,128)S(1)} copy-done((f32[128,128]{1,0:T(8,128)S(1)}, f32[128,128]{1,0:T(8,128)}, u32[]{:S(2)}) %copy-start.1) | copy-done | bytes 65560
  39.6 11.5 %apply.1 = (f32[128,64,256]{2,1,0:T(8,128)}, f32[128,128]{1,0:T(8,128)}) custom-call(f32[128,128]{1,0:T(8,128)S(1)} %copy-done.1, bf16[256,16384]{1,0:T(8,128)(2,1)S(1)} %copy-done), custom_call_target="tpu_custom_call" | custom-call | tf_op jit(solution)/shard_map/apply/pallas_call | solution.py:285
Async XLA Ops:
  35.4 3.4 %copy-start = (bf16[256,16384]{1,0:T(8,128)(2,1)S(1)}, bf16[256,16384]{1,0:T(8,128)(2,1)}, u32[]{:S(2)}) copy-start(bf16[256,16384]{1,0:T(8,128)(2,1)} %get-tuple-element.5.m_ref) | copy-start | bytes 25165828
  38.8 0.8 %copy-start.1 = (f32[128,128]{1,0:T(8,128)S(1)}, f32[128,128]{1,0:T(8,128)}, u32[]{:S(2)}) copy-start(f32[128,128]{1,0:T(8,128)} %get-tuple-element.4.g_ref) | copy-start | bytes 196612

commit v3 on v2

--- a/solution.py
+++ b/solution.py
@@ -23,17 +23,21 @@
     halo_send, halo_recv, rs_send, rs_recv, all_send, all_recv, ag_send, ag_recv,
 ):
     rows, cols = k_hbm.shape
-    modes = u_hbm.shape[0] // rows
+    modes = u_hbm.shape[0]
     tiles = cols // 128
     columns = 4 * modes
     share = columns // ny
     px, py = lax.axis_index("gx"), lax.axis_index("gy")
 
     loads = [
-        pltpu.make_async_copy(u_hbm.at[:, pl.ds(t * 128, 128)], flat.at[t], load.at[t]) for t in range(tiles)
-    ]
-    loads.append(pltpu.make_async_copy(k_hbm, k_ref, load.at[tiles]))
-    loads.append(pltpu.make_async_copy(p_hbm, p_ref, load.at[tiles + 1]))
+        pltpu.make_async_copy(
+            u_hbm.at[:, pl.ds(q * 8, 8), pl.ds(t * 128, 128)], flat.at[t, q], load.at[t * (rows // 8) + q]
+        )
+        for q in range(rows // 8)
+        for t in range(tiles)
+    ]
+    loads.append(pltpu.make_async_copy(k_hbm, k_ref, load.at[tiles * rows // 8]))
+    loads.append(pltpu.make_async_copy(p_hbm, p_ref, load.at[tiles * rows // 8 + 1]))
     for copy in loads:
         copy.start()
     barrier = pltpu.get_barrier_semaphore()
@@ -44,21 +48,25 @@
 
     lanes = lax.broadcasted_iota(jnp.int32, (modes + 8, 128), 1)
 
-    def spread(i, carry):
+    blocks = flat.reshape(tiles, rows // 8, modes * 8, 128)
+
+    def spread(q, carry):
         first, last = carry
-        row = jnp.concatenate(
-            [jnp.concatenate([flat[t, pl.ds(i, modes, stride=rows), :] for t in range(tiles)], 1),
-             jnp.broadcast_to(k_ref[pl.ds(i, 1), :], (8, cols))], 0
-        )
-        wide[i + 1] = row
-        first = jnp.where(lanes == i, pltpu.roll(row[:, :128], i, 1), first)
-        last = jnp.where(lanes == i, pltpu.roll(row[:, cols - 128:], lax.rem(i + 1, 128), 1), last)
+        for s in range(8):
+            i = q * 8 + s
+            row = jnp.concatenate(
+                [jnp.concatenate([blocks[t, q, pl.ds(s, modes, stride=8), :] for t in range(tiles)], 1),
+                 jnp.broadcast_to(k_ref[pl.ds(i, 1), :], (8, cols))], 0
+            )
+            wide[i + 1] = row
+            first = jnp.where(lanes == i, pltpu.roll(row[:, :128], i, 1), first)
+            last = jnp.where(lanes == i, pltpu.roll(row[:, cols - 128:], lax.rem(i + 1, 128), 1), last)
         return first, last
 
     for copy in loads:
         copy.wait()
     zero = jnp.zeros((modes + 8, 128), F32)
-    first, last = lax.fori_loop(0, rows, spread, (zero, zero), unroll=4)
+    first, last = lax.fori_loop(0, rows // 8, spread, (zero, zero))
     edge[0] = first
     edge[1] = last
 
@@ -177,16 +185,16 @@
     return pl.pallas_call(
         functools.partial(gram_kernel, nx, ny),
         out_shape=(
-            jax.ShapeDtypeStruct((2 * columns, rows * cols), BF16),
-            jax.ShapeDtypeStruct((columns, columns), F32),
+            pltpu.VMEM((2 * columns, rows * cols), BF16),
+            pltpu.VMEM((columns, columns), F32),
         ),
         in_specs=[pl.BlockSpec(memory_space=pltpu.HBM)] * 3,
         out_specs=(vmem, vmem),
         scratch_shapes=[
             pltpu.VMEM((rows, cols), F32),
             pltpu.VMEM((rows, cols), F32),
-            pltpu.VMEM((cols // 128, modes * rows, 128), F32),
-            dma((cols // 128 + 2,)),
+            pltpu.VMEM((cols // 128, rows // 8, modes, 8, 128), F32),
+            dma((cols // 128 * rows // 8 + 2,)),
             pltpu.VMEM((rows + 2, modes + 8, cols), F32),
             pltpu.VMEM((2, modes + 8, 128), F32),
             pltpu.VMEM((2, modes + 8, 128), F32),
@@ -198,10 +206,10 @@
             dma((4,)), dma((4,)), dma((ny,)), dma((ny,)), dma((nx,)), dma((nx,)), dma((ny,)), dma((ny,)),
         ],
         compiler_params=pltpu.CompilerParams(
-            collective_id=0, has_side_effects=True, vmem_limit_bytes=66_900_000 - 4 * columns * rows * cols
+            collective_id=0, has_side_effects=True, vmem_limit_bytes=28 * 1024 * 1024
         ),
         name="gram",
-    )(fields.reshape(modes * rows, cols), conduct, potential)
+    )(*(pltpu.with_memory_space_constraint(a, pltpu.HBM) for a in (fields, conduct, potential)))
 
 
 def factor(g_ref, r_ref, w_ref):
@@ -279,7 +287,7 @@
 
 def apply(total, matrix, rows, cols):
     columns = total.shape[0]
-    chunk = 16
+    chunk = 8
     steps = rows // chunk
     square = pl.BlockSpec((columns, columns), lambda t, i: (0, 0))
     return pl.pallas_call(

time: 51.4 us -> 45.3 us (0.88)
  local copies, waits for them, and re-layouts: 4.21 us -> 0 us
  Pallas kernels: 46.3 us -> 44.5 us
    pallas_call x1, Pallas kernels: 34.7 us -> 30.3 us  [gram(): pl.pallas_call(functools.partial(gram_kernel, nx, ny), out_shape=(pltpu.V...]
    unnamed x4 -> x0, local copies, waits for them, and re-layouts: 4.21 us -> none
    pallas_call x1, Pallas kernels: 11.5 us -> 14.2 us  [apply(): pl.pallas_call(apply_kernel, out_shape=(jax.ShapeDtypeStruct((columns, ro...]
where the time goes in v3:
time: 45.3 us; the launch traced here: 45.2 us
  Pallas kernels  44.5 us (98%)
  between operations  0.64 us (1%)
    pallas_call x1, Pallas kernels, gram(): pl.pallas_call(functools.partial(gram_kernel, nx, ny), out_shape=(pltpu.V...  30.3 us
    pallas_call x1, Pallas kernels, apply(): pl.pallas_call(apply_kernel, out_shape=(jax.ShapeDtypeStruct((columns, ro...  14.2 us

profile of v3, /device:TPU:0, one launch (start us, length us, event | category | flops | bytes accessed | tf_op | source)
XLA Modules:
  0.0 45.2 jit_solution(5102337668199219595)
XLA Ops:
  0.6 30.3 %gram.1 = (bf16[256,16384]{1,0:T(8,128)(2,1)S(1)}, f32[128,128]{1,0:T(8,128)S(1)}) custom-call(f32[32,64,256]{2,1,0:T(8,128)} %u_hbm.1, f32[64,256]{1,0:T(8,128)} %k_hbm.1, f32[64,256]{1,0:T(8,128)} %p_hbm.1), custom_call_target="tpu_custom_call" | custom-call | tf_op jit(solution)/shard_map/gram/pallas_call | solution.py:185
  31.0 14.2 %apply.1 = (f32[128,64,256]{2,1,0:T(8,128)}, f32[128,128]{1,0:T(8,128)}) custom-call(f32[128,128]{1,0:T(8,128)S(1)} %get-tuple-element.4.g_ref, bf16[256,16384]{1,0:T(8,128)(2,1)S(1)} %get-tuple-element.5.m_ref), custom_call_target="tpu_custom_call" | custom-call | tf_op jit(solution)/shard_map/apply/pallas_call | solution.py:293

commit v4 on v3

--- a/solution.py
+++ b/solution.py
@@ -265,44 +265,61 @@
                 z[i] = jnp.where(inside, 0.0, z[i]) - functools.reduce(jnp.add, terms)
 
 
-def apply_kernel(g_ref, m_ref, o_ref, r_ref, w_ref, weights):
-    columns, chunk, _ = o_ref.shape
-
-    @pl.when((pl.program_id(0) == 0) & (pl.program_id(1) == 0))
-    def _():
-        factor(g_ref, r_ref, w_ref)
-        high, low = split(w_ref[...])
-        weights[:columns, :columns] = high
-        weights[:columns, columns:] = high
-        weights[columns:, :columns] = low
-        weights[columns:, columns:] = jnp.zeros_like(low)
-
-    flat = o_ref.reshape(columns * chunk, 128)
-    for s in range(0, chunk, 2):
-        both = jnp.dot(weights[...], m_ref[:, s * 128:(s + 2) * 128], preferred_element_type=F32)
-        out = both[:columns] + both[columns:]
-        for r in range(2):
-            flat[pl.ds(s + r, columns, stride=chunk), :] = out[:, r * 128:(r + 1) * 128]
+def apply_kernel(g_ref, m_ref, o_hbm, r_ref, w_ref, weights, out, sent):
+    parts, columns, chunk, _ = out.shape
+    per = o_hbm.shape[1] // chunk
+    factor(g_ref, r_ref, w_ref)
+    high, low = split(w_ref[...])
+    weights[:columns, :columns] = high
+    weights[:columns, columns:] = high
+    weights[columns:, :columns] = low
+    weights[columns:, columns:] = jnp.zeros_like(low)
+    flat = out.reshape(parts, columns * chunk, 128)
+
+    def send(q):
+        to = o_hbm.at[:, pl.ds(lax.rem(q, per) * chunk, chunk), pl.ds(pl.multiple_of(q // per * 128, 128), 128)]
+        return pltpu.make_async_copy(out.at[q], to, sent.at[q])
+
+    def step(q, _):
+        for s in range(0, chunk, 2):
+            at = pl.ds(pl.multiple_of((q * chunk + s) * 128, 256), 256)
+            both = jnp.dot(weights[...], m_ref[:, at], preferred_element_type=F32)
+            value = both[:columns] + both[columns:]
+            for r in range(2):
+                flat[q, pl.ds(s + r, columns, stride=chunk), :] = value[:, r * 128:(r + 1) * 128]
+        send(q).start()
+        return 0
+
+    def finish(q, _):
+        send(q).wait()
+        return 0
+
+    lax.fori_loop(0, parts, step, 0)
+    lax.fori_loop(0, parts, finish, 0)
 
 
 def apply(total, matrix, rows, cols):
     columns = total.shape[0]
     chunk = 8
-    steps = rows // chunk
-    square = pl.BlockSpec((columns, columns), lambda t, i: (0, 0))
+    parts = (rows // chunk) * (cols // 128)
+    vmem = pl.BlockSpec(memory_space=pltpu.VMEM)
     return pl.pallas_call(
         apply_kernel,
         out_shape=(
             jax.ShapeDtypeStruct((columns, rows, cols), F32),
             jax.ShapeDtypeStruct((columns, columns), F32),
         ),
-        grid=(cols // 128, steps),
-        in_specs=[square, pl.BlockSpec((2 * columns, chunk * 128), lambda t, i: (0, t * steps + i))],
-        out_specs=(pl.BlockSpec((columns, chunk, 128), lambda t, i: (0, i, t)), square),
-        scratch_shapes=[pltpu.VMEM((columns, columns), F32), pltpu.VMEM((2 * columns, 2 * columns), BF16)],
-        compiler_params=pltpu.CompilerParams(vmem_limit_bytes=16 * 1024 * 1024),
+        in_specs=[vmem, vmem],
+        out_specs=(pl.BlockSpec(memory_space=pltpu.HBM), vmem),
+        scratch_shapes=[
+            pltpu.VMEM((columns, columns), F32),
+            pltpu.VMEM((2 * columns, 2 * columns), BF16),
+            pltpu.VMEM((parts, columns, chunk, 128), F32),
+            pltpu.SemaphoreType.DMA((parts,)),
+        ],
+        compiler_params=pltpu.CompilerParams(vmem_limit_bytes=20 * 1024 * 1024),
         name="apply",
-    )(total, matrix)
+    )(total, pltpu.with_memory_space_constraint(matrix, pltpu.VMEM))
 
 
 def on_device(nx, ny, mode_fields, conductance, potential):

time: 45.3 us -> 42.4 us (0.936)
  Pallas kernels: 44.5 us -> 41.7 us
    pallas_call x1, Pallas kernels: 14.2 us -> 11.3 us  [apply(): pl.pallas_call(apply_kernel, out_shape=(jax.ShapeDtypeStruct((columns, ro...]
where the time goes in v4:
time: 42.4 us; the launch traced here: 42.3 us
  Pallas kernels  41.7 us (98%)
  between operations  0.64 us (2%)
    pallas_call x1, Pallas kernels, gram(): pl.pallas_call(functools.partial(gram_kernel, nx, ny), out_shape=(pltpu.V...  30.3 us
    pallas_call x1, Pallas kernels, apply(): pl.pallas_call(apply_kernel, out_shape=(jax.ShapeDtypeStruct((columns, ro...  11.3 us

profile of v4, /device:TPU:0, one launch (start us, length us, event | category | flops | bytes accessed | tf_op | source)
XLA Modules:
  0.0 42.3 jit_solution(16510508666322547384)
XLA Ops:
  0.6 30.3 %gram.1 = (bf16[256,16384]{1,0:T(8,128)(2,1)S(1)}, f32[128,128]{1,0:T(8,128)S(1)}) custom-call(f32[32,64,256]{2,1,0:T(8,128)} %u_hbm.1, f32[64,256]{1,0:T(8,128)} %k_hbm.1, f32[64,256]{1,0:T(8,128)} %p_hbm.1), custom_call_target="tpu_custom_call" | custom-call | tf_op jit(solution)/shard_map/gram/pallas_call | solution.py:185
  31.0 11.3 %apply.1 = (f32[128,64,256]{2,1,0:T(8,128)}, f32[128,128]{1,0:T(8,128)}) custom-call(f32[128,128]{1,0:T(8,128)S(1)} %get-tuple-element.4.g_ref, bf16[256,16384]{1,0:T(8,128)(2,1)S(1)} %get-tuple-element.5.m_ref), custom_call_target="tpu_custom_call" | custom-call | tf_op jit(solution)/shard_map/apply/pallas_call | solution.py:306
